TPU v7x, 32 devices: a whole 2x2x4 slice. The times are simulated.
32 devices in a mesh: lat: 4 (over y, x), lon: 8 (over z, core).
Axes of the slice: x: 2, y: 2, z: 4, core: 2. Of those that a mesh axis runs over, the one named last changes fastest.
Arguments:
- latent_field: bfloat16 [640, 32, 64], P(None, 'lat', 'lon'), may hold values from -6 to 6
- spectral_filter: float32 [640, 32], P('lon'), may hold values from -5 to 5
- conv_weight: float32 [9, 640], replicated, may hold values from -2 to 2
- norm_gain: float32 [640], replicated, may hold values from 0.1 to 1.9
- weight_in: bfloat16 [640, 1280], replicated, may hold values from -0.25 to 0.25
- weight_out: bfloat16 [1280, 640], replicated, may hold values from -0.15625 to 0.15625
Outputs:
- updated: bfloat16 [640, 32, 64], P(None, 'lat', 'lon')
All inputs are finite; a program needn't handle non-finite values.
Results may differ from a plain program's by a relative error of at most 0.01.
Values may be sent and summed in bfloat16 or wider, within the bound.
A program may use at most 128 MiB of HBM per device.

v0:
```python
import functools
import math

import jax
import jax.numpy as jnp
import numpy as np
from jax import lax
from jax.experimental import pallas as pl
from jax.experimental.pallas import tpu as pltpu
from jax.sharding import PartitionSpec as P

highest = lax.Precision.HIGHEST
epsilon_norm = 1e-06


def with_halo(cells, sides, width):
    for axis, dim in sides:
        count = lax.axis_size(axis)
        ends = count - 1
        head = lax.slice_in_dim(cells, 0, width, axis=dim)
        tail = lax.slice_in_dim(cells, cells.shape[dim] - width, cells.shape[dim], axis=dim)
        cells = jnp.concatenate(
            [
                lax.ppermute(tail, axis, [(i, (i + 1) % count) for i in range(ends)]),
                cells,
                lax.ppermute(head, axis, [((i + 1) % count, i) for i in range(ends)]),
            ],
            axis=dim,
        )
    return cells


def quadrature(lat_count):
    colatitude = (jnp.arange(lat_count, dtype=jnp.float32) + 0.5) * (math.pi / lat_count)
    return jnp.sin(colatitude) * (math.pi / lat_count)


def fourier_tables(lon_count, mode_count):
    wave_index = (
        jnp.arange(mode_count, dtype=jnp.int32)[:, None]
        * jnp.arange(lon_count, dtype=jnp.int32)[None, :]
    )
    phase_angle = (wave_index % lon_count).astype(jnp.float32) * (2.0 * math.pi / lon_count)
    cosine = jnp.cos(phase_angle)
    sine_table = jnp.sin(phase_angle)
    angle_step = 2.0 * math.pi / lon_count
    forward = jnp.concatenate([angle_step * cosine, -angle_step * sine_table], axis=0)
    weight = jnp.where(jnp.arange(mode_count, dtype=jnp.int32) == 0, 1.0, 2.0).astype(jnp.float32)[
        :, None
    ]
    inverse = jnp.concatenate([weight * cosine, -weight * sine_table], axis=0)
    return (forward, inverse)


def legendre_rows(order_ids, lat_count):
    colatitude = (jnp.arange(lat_count, dtype=jnp.float32) + 0.5) * (math.pi / lat_count)
    cosine = jnp.cos(colatitude)
    sine_col = jnp.sin(colatitude)
    order_f = order_ids.astype(jnp.float32)
    factor_index = jnp.arange(1, lat_count, dtype=jnp.float32)
    ratio_log = jnp.log((2.0 * factor_index - 1.0) / (2.0 * factor_index))
    included = (factor_index[None, :] <= order_f[:, None]).astype(jnp.float32)
    log_factor = jnp.sum(included * ratio_log[None, :], axis=1)
    start_log = 0.5 * jnp.log((2.0 * order_f + 1.0) / (4.0 * math.pi)) + 0.5 * log_factor
    start_log = start_log[:, None] + order_f[:, None] * jnp.log(sine_col)[None, :]
    blank_rows = jnp.zeros((order_ids.shape[0], lat_count), jnp.float32)
    order_col = order_f[:, None]

    def advance(state_carry, degree):
        before, current, scale_log = state_carry
        degree_f = degree.astype(jnp.float32)
        alpha_term = jnp.sqrt(
            (4.0 * degree_f * degree_f - 1.0)
            / jnp.maximum(degree_f * degree_f - order_col * order_col, 1.0)
        )
        beta_term = jnp.sqrt(
            jnp.maximum((degree_f - 1.0) ** 2 - order_col * order_col, 0.0)
            / jnp.maximum(4.0 * (degree_f - 1.0) ** 2 - 1.0, 1.0)
        )
        stepped = alpha_term * (cosine[None, :] * current - beta_term * before)
        at_start = order_ids[:, None] == degree
        past_start = order_ids[:, None] < degree
        fresh_value = jnp.where(at_start, 1.0, jnp.where(past_start, stepped, 0.0))
        fresh_log = jnp.where(at_start, start_log, scale_log)
        entry_value = fresh_value * jnp.exp(fresh_log)
        rescale = jnp.where(
            past_start | at_start, jnp.maximum(jnp.abs(fresh_value), jnp.abs(current)), 1.0
        )
        return (
            (current / rescale, fresh_value / rescale, fresh_log + jnp.log(rescale)),
            entry_value,
        )

    degrees = jnp.arange(lat_count, dtype=jnp.int32)
    unused, legendre = lax.scan(advance, (blank_rows, blank_rows, blank_rows), degrees)
    return legendre


def filter_modes(banded, legendre, filter_block, quad_weights):
    coefficients = jnp.einsum(
        "lmj,pmcj->pmcl", legendre, banded * quad_weights[None, None, None, :], precision=highest
    )
    coefficients = coefficients * filter_block[None, None, :, :]
    return jnp.einsum("lmj,pmcl->pmcj", legendre, coefficients, precision=highest)


def wrap_columns(extended):
    return jnp.concatenate([extended[:, :, -1:], extended, extended[:, :, :1]], axis=2)


def depthwise_core(extended, kernel, lat_rows, lon_cols):
    accumulated = jnp.zeros((extended.shape[0], lat_rows, lon_cols), jnp.float32)
    for row_shift in range(3):
        for col_shift in range(3):
            piece = extended[
                :, row_shift : row_shift + lat_rows, col_shift : col_shift + lon_cols
            ].astype(jnp.float32)
            accumulated = accumulated + kernel[3 * row_shift + col_shift][:, None, None] * piece
    return accumulated.astype(jnp.bfloat16)


def channel_mlp(summed_low, norm_gain, weight_in, weight_out):
    summed = summed_low.astype(jnp.float32)
    scale_inv = lax.rsqrt(jnp.mean(summed * summed, axis=0, keepdims=True) + epsilon_norm)
    normed = (summed * scale_inv * norm_gain[:, None]).astype(jnp.bfloat16)
    hidden = lax.dot_general(
        weight_in, normed, (((0,), (0,)), ((), ())), preferred_element_type=jnp.float32
    )
    hidden = jax.nn.gelu(hidden, approximate=False).astype(jnp.bfloat16)
    result = summed + lax.dot_general(
        weight_out, hidden, (((0,), (0,)), ((), ())), preferred_element_type=jnp.float32
    )
    return result.astype(jnp.bfloat16)


def add_three(first, second, third):
    total = first.astype(jnp.float32) + second.astype(jnp.float32) + third.astype(jnp.float32)
    return total.astype(jnp.bfloat16)


def on_device(latent_field, spectral_filter, conv_weight, norm_gain, weight_in, weight_out):
    channels, lat_rows, lon_cols = latent_field.shape
    sector_count = lax.axis_size("lon")
    lat_count = lat_rows * lax.axis_size("lat")
    lon_count = lon_cols * sector_count
    chan_block = channels // sector_count
    spread = lax.all_to_all(latent_field, "lon", split_axis=0, concat_axis=2, tiled=True)
    forward, inverse = fourier_tables(lon_count, lat_count)
    flattened = spread.astype(jnp.float32).reshape(chan_block * lat_rows, lon_count)
    spectrum = lax.dot_general(forward, flattened, (((1,), (1,)), ((), ())), precision=highest)
    spectrum = spectrum.reshape(2, lat_count, chan_block, lat_rows)
    banded = lax.all_to_all(spectrum, "lat", split_axis=1, concat_axis=3, tiled=True)
    order_ids = lax.axis_index("lat") * lat_rows + jnp.arange(lat_rows, dtype=jnp.int32)
    legendre = legendre_rows(order_ids, lat_count)
    synthesized = filter_modes(banded, legendre, spectral_filter, quadrature(lat_count))
    regathered = lax.all_to_all(synthesized, "lat", split_axis=3, concat_axis=1, tiled=True)
    regridded = lax.dot_general(
        regathered.reshape(2 * lat_count, chan_block * lat_rows),
        inverse,
        (((0,), (0,)), ((), ())),
        precision=highest,
    )
    spectral = regridded.reshape(chan_block, lat_rows, lon_count).astype(jnp.bfloat16)
    own_kernel = lax.dynamic_slice_in_dim(
        conv_weight, lax.axis_index("lon") * chan_block, chan_block, 1
    )
    rimmed = with_halo(spread, (("lat", 1),), 1)
    sector_mix = depthwise_core(wrap_columns(rimmed), own_kernel, lat_rows, lon_count)
    sector_sum = add_three(spread, spectral, sector_mix)
    summed = lax.all_to_all(sector_sum, "lon", split_axis=2, concat_axis=0, tiled=True)
    summed = summed.reshape(channels, lat_rows * lon_cols)
    result = channel_mlp(summed, norm_gain, weight_in, weight_out)
    return result.reshape(channels, lat_rows, lon_cols)


CLASSES = ((0, 0), (1, 0), (0, 1), (1, 1))


def folded_tables(lat_devices, lon_devices, lat_rows, lon_cols):
    lat_count, lon_count = lat_devices * lat_rows, lon_devices * lon_cols
    theta = (np.arange(lat_count // 2) + 0.5) * (math.pi / lat_count)
    x, s = np.cos(theta), np.sin(theta)
    phi = 2.0 * math.pi * (np.arange(lon_count // 2) + 0.5) / lon_count
    row, column = [], []
    for b in reversed(range(lon_devices // 2)):
        for a in range(lat_devices // 2):
            row.append(np.repeat(a * lat_rows + np.arange(lat_rows), lon_cols))
            column.append(np.tile(b * lon_cols + np.arange(lon_cols), lat_rows))
    row, column = np.concatenate(row), np.concatenate(column)
    columns = {key: [] for key in CLASSES}
    degrees = {key: [] for key in CLASSES}
    weights = {key: [] for key in CLASSES}
    for m in range(lat_count):
        k = np.arange(1, m + 1)
        log_start = 0.5 * (
            np.log((2 * m + 1) / (4 * math.pi)) + np.sum(np.log((2 * k - 1) / (2 * k)))
        )
        before, current = np.zeros(lat_count // 2), np.exp(log_start + m * np.log(s))
        for l in range(m, lat_count):
            if l > m:
                a = math.sqrt((4.0 * l * l - 1) / (l * l - m * m))
                b = math.sqrt(((l - 1.0) ** 2 - m * m) / (4.0 * (l - 1) ** 2 - 1))
                before, current = current, a * (x * current - b * before)
            for phase, wave in enumerate([np.cos(m * phi), -np.sin(m * phi)][: 1 if m == 0 else 2]):
                key = ((l + m) % 2, phase)
                columns[key].append(current[row] * wave[column])
                degrees[key].append(l)
                weights[key].append((1.0 if m == 0 else 2.0) * 2.0 * math.pi / lon_count)
    tables, selects, starts = [], [], [0]
    for key in CLASSES:
        width = -(-len(columns[key]) // 128) * 128
        fill = width - len(columns[key])
        tables.append(np.pad(np.stack(columns[key], 1), ((0, 0), (0, fill))))
        select = np.arange(lat_count)[:, None] == np.array(degrees[key])[None, :]
        selects.append(np.pad(select * np.array(weights[key])[None, :], ((0, 0), (0, fill))))
        starts.append(starts[-1] + width)
    quad = s * (math.pi / lat_count)
    quad = np.repeat(quad.reshape(lat_devices // 2, lat_rows), lon_cols, axis=1)
    return (
        np.concatenate(tables, 1),
        np.concatenate(selects, 1).astype(np.float32),
        np.tile(quad, (1, 2)).astype(np.float32),
        tuple(starts),
    )


MESH = pl.DeviceIdType.MESH
NT = (((1,), (1,)), ((), ()))


def upper_rows(own):
    return -(-(own // 2) // 8) * 8


def block_kernel(
    lat_devices, lon_devices, lat_rows, lon_cols, starts,
    x_hbm, filter_hbm, taps_hbm, norm_hbm, win_hbm, wout_hbm, table_hbm, select_hbm, quad_hbm,
    out_hbm,
    xb, filt, taps, norm, win, wout, table, select, quad,
    xf, src, mid, out, dst, filt_in, edge_out, corner_out, edge_in, corner_in, total, res,
    local_sem, send1, recv1, send2, recv2, halo_send, halo_recv, filt_send, filt_recv,
):
    A, B = lat_devices, lon_devices
    A2, B2, first = A // 2, B // 2, B // 4
    workers = A * B2
    devices = A * B
    points, channels = xb.shape
    own = channels // workers
    up = upper_rows(own)
    low = own - up
    half = points
    a, b = lax.axis_index("lat"), lax.axis_index("lon")
    me = b * A + a
    worker = jnp.logical_and(b >= first, b < first + B2)
    mine = jnp.where(worker, (b - first) * A + a, -1)
    f32, bf16 = jnp.float32, jnp.bfloat16

    fetch = [
        pltpu.make_async_copy(s, d, local_sem.at[i])
        for i, (s, d) in enumerate(
            [(x_hbm, xb), (filter_hbm, filt), (quad_hbm, quad), (table_hbm, table), (select_hbm, select),
             (taps_hbm, taps), (norm_hbm, norm), (win_hbm, win), (wout_hbm, wout)]
        )
    ]
    fetch[0].start()
    barrier = pltpu.get_barrier_semaphore()
    neighbours = [(da, db) for da in (-1, 0, 1) for db in (-1, 0, 1) if (da, db) != (0, 0)]

    def inside(da):
        return jnp.logical_and(a + da >= 0, a + da < A)

    def at(da, db):
        return (a + da, lax.rem(b + db + B, B))

    @pl.when(worker)
    def _():
        def greet(step, carry):
            peer = lax.rem(me + step, devices)
            pl.semaphore_signal(
                barrier, inc=1, device_id=(lax.rem(peer, A), lax.div(peer, A)), device_id_type=MESH
            )
            return carry

        lax.fori_loop(1, devices, greet, 0)

    @pl.when(jnp.logical_not(worker))
    def _():
        for da, db in neighbours:
            @pl.when(inside(da))
            def _():
                pl.semaphore_signal(barrier, inc=1, device_id=at(da, db), device_id_type=MESH)

    for copy in fetch[1:]:
        copy.start()

    turn_lat, turn_lon = a >= A2, b >= B2
    p_row = lax.broadcasted_iota(jnp.int32, (points, 2 * half), 0)
    p_col = lax.broadcasted_iota(jnp.int32, (points, 2 * half), 1)

    def turned(index):
        jl, kl = lax.div(index, lon_cols), lax.rem(index, lon_cols)
        jl = jnp.where(turn_lat, lat_rows - 1 - jl, jl)
        kl = jnp.where(turn_lon, lon_cols - 1 - kl, kl)
        return jl * lon_cols + kl

    place = jnp.where(p_row == turned(lax.rem(p_col, half)), 1.0, 0.0)
    place_both = place.astype(bf16)
    place_left = jnp.where(p_col < half, place, 0.0).astype(bf16)
    lane = lax.broadcasted_iota(jnp.int32, (up, 2 * half), 1)
    left = lane < half

    fetch[0].wait()
    xf[...] = xb[...].astype(f32)
    xt = jnp.transpose(xf[...], (1, 0)).astype(bf16)
    xt = jnp.dot(xt, place_both, preferred_element_type=f32)
    blank = jnp.zeros((up - low, 2 * half), f32)
    for g in range(workers):
        upper = xt[own * g : own * g + up]
        lower = jnp.concatenate([xt[own * g + up : own * (g + 1)], blank], 0)
        src[g] = jnp.where(left, upper, lower).astype(bf16)

    @pl.when(worker)
    def _():
        mid[me] = src[mine]

    west, east = [
        jnp.concatenate([xf[k + lon_cols * r : k + lon_cols * r + 1] for r in range(lat_rows)], 0)
        for k in (0, lon_cols - 1)
    ]
    edge_out[0] = west.astype(bf16)
    edge_out[1] = east.astype(bf16)
    chunks = channels // 128
    for i, (r, side) in enumerate([(0, west), (0, east), (lat_rows - 1, west), (lat_rows - 1, east)]):
        parts = [side[r : r + 1, 128 * c : 128 * (c + 1)] for c in range(chunks)]
        parts.append(jnp.zeros((8 - chunks, 128), f32))
        corner_out[i] = jnp.concatenate(parts, 0).astype(bf16)

    def outside(db):
        other = lax.rem(b + db + B, B)
        return jnp.where(jnp.logical_and(other >= first, other < first + B2), 0, 1)

    rims = jnp.where(a > 0, 1, 0) + jnp.where(a < A - 1, 1, 0)
    greetings = jnp.where(worker, workers - 1, workers)
    greetings = greetings + rims * outside(0) + (1 + rims) * (outside(-1) + outside(1))
    pl.semaphore_wait(barrier, greetings)

    def first_copy(g):
        return pltpu.make_async_remote_copy(
            src_ref=src.at[g], dst_ref=mid.at[me], send_sem=send1.at[g], recv_sem=recv1.at[me],
            device_id=(lax.rem(g, A), first + lax.div(g, A)), device_id_type=MESH,
        )

    def first_send(step, carry):
        g = lax.rem(me + step, workers)

        @pl.when(g != mine)
        def _():
            first_copy(g).start()

        return carry

    lax.fori_loop(0, workers, first_send, 0)

    fetch[1].wait()
    owner_row = lax.div(a, A2) == lax.rem(b, 2)
    filt_lon = first + lax.div(b, 2)
    keeps = jnp.logical_and(owner_row, filt_lon == b)
    gives = jnp.logical_and(owner_row, filt_lon != b)
    filt_copy = pltpu.make_async_remote_copy(
        src_ref=filt, dst_ref=filt_in, send_sem=filt_send, recv_sem=filt_recv,
        device_id=(a, filt_lon), device_id_type=MESH,
    )

    @pl.when(gives)
    def _():
        filt_copy.start()

    @pl.when(keeps)
    def _():
        filt_in[...] = filt[...]

    def halo_copy(da, db):
        if db == 0:
            row = 0 if da < 0 else points - lon_cols
            source, target = xb.at[pl.ds(row, lon_cols)], edge_in.at[1 if da < 0 else 0]
            slot = 1 if da < 0 else 0
        elif da == 0:
            slot = 3 if db < 0 else 2
            source, target = edge_out.at[0 if db < 0 else 1], edge_in.at[slot]
        else:
            index = (0 if da < 0 else 2) + (0 if db < 0 else 1)
            source, target = corner_out.at[index], corner_in.at[3 - index]
            slot = 4 + 3 - index
        return pltpu.make_async_remote_copy(
            src_ref=source, dst_ref=target, send_sem=halo_send.at[slot], recv_sem=halo_recv.at[slot],
            device_id=at(da, db), device_id_type=MESH,
        )

    for da, db in neighbours:
        @pl.when(inside(da))
        def _():
            halo_copy(da, db).start()

    def index_of(ai, bi):
        return bi * A + ai

    def first_wait(o, carry):
        @pl.when(o != me)
        def _():
            pltpu.make_async_remote_copy(
                src_ref=src.at[0], dst_ref=mid.at[o], send_sem=send1.at[0], recv_sem=recv1.at[o],
                device_id=(lax.rem(o, A), lax.div(o, A)), device_id_type=MESH,
            ).wait_recv()

        return carry

    def widths(c):
        return pl.ds(starts[c], starts[c + 1] - starts[c])

    def folded(bs):
        tiles = [[] for _ in CLASSES]
        for bi in bs:
            parts = []
            for ai in range(A2):
                f00, f10, f01, f11 = [
                    mid[index_of(i, j)].astype(f32)
                    for i, j in [(ai, bi), (A - 1 - ai, bi), (ai, B - 1 - bi), (A - 1 - ai, B - 1 - bi)]
                ]
                s0, d0, s1, d1 = f00 + f10, f00 - f10, f01 + f11, f01 - f11
                w = quad[ai : ai + 1, :]
                parts.append([(s0 + s1) * w, (d0 + d1) * w, (s0 - s1) * w, (d0 - d1) * w])
            for ai in range(0, A2, 2):
                for c in range(4):
                    u, v = parts[ai][c], parts[ai + 1][c]
                    upper = jnp.where(left, u, pltpu.roll(v, half, 1))
                    lower = jnp.where(left, pltpu.roll(u, half, 1), v)
                    tiles[c].append(jnp.concatenate([upper, lower[:low]], 0).astype(bf16))
        return [jnp.concatenate(t, 1) for t in tiles]

    inner = tuple(reversed(range(B2 // 2, B2)))
    outer = tuple(reversed(range(B2 // 2)))
    rows_of = lambda bs: pl.ds((B2 - 1 - bs[0]) * A2 * half, len(bs) * A2 * half)

    def second_copy(o):
        return pltpu.make_async_remote_copy(
            src_ref=out.at[o], dst_ref=dst.at[mine], send_sem=send2.at[o], recv_sem=recv2.at[mine],
            device_id=(lax.rem(o, A), lax.div(o, A)), device_id_type=MESH,
        )

    @pl.when(worker)
    def _():
        for i in (2, 3, 4):
            fetch[i].wait()

        @pl.when(jnp.logical_not(keeps))
        def _():
            pltpu.make_async_remote_copy(
                src_ref=filt, dst_ref=filt_in, send_sem=filt_send, recv_sem=filt_recv,
                device_id=(a, 2 * (b - first) + lax.div(a, A2)), device_id_type=MESH,
            ).wait_recv()

        held = filt_in.shape[1]
        r = lax.broadcasted_iota(jnp.int32, (own, held), 0)
        c = lax.broadcasted_iota(jnp.int32, (own, held), 1)
        pick = jnp.where(c == r + lax.rem(a, A2) * own, 1.0, 0.0)
        rows = lax.dot_general(pick, filt_in[...], NT, precision=highest, preferred_element_type=f32)
        gain = jnp.dot(rows, select[...], precision=highest, preferred_element_type=f32)

        lax.fori_loop(A * inner[-1], A * (B - inner[-1]), first_wait, 0)
        acc = [
            jnp.dot(t, table[rows_of(inner), widths(i)], preferred_element_type=f32)
            for i, t in enumerate(folded(inner))
        ]
        lax.fori_loop(0, A * inner[-1], first_wait, 0)
        lax.fori_loop(A * (B - inner[-1]), devices, first_wait, 0)
        for i, t in enumerate(folded(outer)):
            acc[i] = acc[i] + jnp.dot(t, table[rows_of(outer), widths(i)], preferred_element_type=f32)
        coef = [(acc[i] * gain[:, starts[i] : starts[i + 1]]).astype(bf16) for i in range(4)]

        for bs in (outer, inner):
            grid = [
                lax.dot_general(coef[i], table[rows_of(bs), widths(i)], NT, preferred_element_type=f32)
                for i in range(4)
            ]
            for n, bi in enumerate(bs):
                for ai in range(0, A2, 2):
                    at_lane = (n * A2 + ai) * half
                    pp, mp, pm, mm = [g[:, at_lane : at_lane + 2 * half] for g in grid]
                    e0, e1, o0, o1 = pp + mp, pp - mp, pm + mm, pm - mm
                    for i, j, value in [(0, 0, e0 + o0), (1, 0, e1 + o1), (0, 1, e0 - o0), (1, 1, e1 - o1)]:
                        upper = value[:up]
                        lower = jnp.concatenate([value[up:], blank], 0)
                        bj = B - 1 - bi if j else bi
                        a0, a1 = (A - 1 - ai, A - 2 - ai) if i else (ai, ai + 1)
                        out[index_of(a0, bj)] = jnp.where(left, upper, pltpu.roll(lower, half, 1)).astype(bf16)
                        out[index_of(a1, bj)] = jnp.where(left, pltpu.roll(upper, half, 1), lower).astype(bf16)

            count = 2 * len(bs) * A

            def second_send(step, carry):
                t = lax.rem(me + step, count)
                if bs == outer:
                    o = t + jnp.where(t >= count // 2, devices - count, 0)
                else:
                    o = t + A * bs[-1]

                @pl.when(o != me)
                def _():
                    second_copy(o).start()

                return carry

            lax.fori_loop(0, count, second_send, 0)
        dst[mine] = out[me]

    @pl.when(a == 0)
    def _():
        edge_in[0] = jnp.zeros(edge_in.shape[1:], bf16)
        corner_in[0] = jnp.zeros(corner_in.shape[1:], bf16)
        corner_in[1] = jnp.zeros(corner_in.shape[1:], bf16)

    @pl.when(a == A - 1)
    def _():
        edge_in[1] = jnp.zeros(edge_in.shape[1:], bf16)
        corner_in[2] = jnp.zeros(corner_in.shape[1:], bf16)
        corner_in[3] = jnp.zeros(corner_in.shape[1:], bf16)

    for da, db in neighbours:
        @pl.when(inside(-da))
        def _():
            halo_copy(da, db).wait_recv()

    fetch[5].wait()
    weight = taps[...]
    grid_rows = [edge_in[0].astype(f32)]
    grid_rows += [xf[pl.ds(lon_cols * r, lon_cols), :] for r in range(lat_rows)]
    grid_rows += [edge_in[1].astype(f32)]

    def corner(i):
        piece = corner_in[i].astype(f32)
        return jnp.concatenate([piece[c : c + 1] for c in range(chunks)], 1)

    west, east = edge_in[2].astype(f32), edge_in[3].astype(f32)
    west = [corner(0)] + [west[r : r + 1] for r in range(lat_rows)] + [corner(2)]
    east = [corner(1)] + [east[r : r + 1] for r in range(lat_rows)] + [corner(3)]
    sub = lax.broadcasted_iota(jnp.int32, (lon_cols, channels), 0)
    shifted = []
    for r in range(lat_rows + 2):
        here = grid_rows[r]
        before = jnp.where(sub == 0, west[r], pltpu.roll(here, 1, 0))
        after = jnp.where(sub == lon_cols - 1, east[r], pltpu.roll(here, lon_cols - 1, 0))
        shifted.append((before, here, after))
    for r in range(lat_rows):
        mix = sum(
            weight[3 * i + j : 3 * i + j + 1] * shifted[r + i][j] for i in range(3) for j in range(3)
        )
        mix = mix.astype(bf16).astype(f32)
        total[pl.ds(lon_cols * r, lon_cols), :] = grid_rows[r + 1] + mix

    for i in (6, 7, 8):
        fetch[i].wait()

    def second_wait(g, carry):
        @pl.when(g != mine)
        def _():
            pltpu.make_async_remote_copy(
                src_ref=out.at[0], dst_ref=dst.at[g], send_sem=send2.at[0], recv_sem=recv2.at[g],
                device_id=(lax.rem(g, A), first + lax.div(g, A)), device_id_type=MESH,
            ).wait_recv()

        return carry

    lax.fori_loop(0, workers, second_wait, 0)
    parts = []
    for g in range(workers):
        piece = dst[g].astype(f32)
        parts += [piece, pltpu.roll(piece, half, 1)[:low]]
    spectral = jnp.concatenate(parts, 0).astype(bf16)
    spectral = lax.dot_general(place_left, spectral, NT, preferred_element_type=f32)
    summed = (total[...] + spectral).astype(bf16).astype(f32)
    scale = lax.rsqrt(jnp.mean(summed * summed, axis=1, keepdims=True) + epsilon_norm)
    normed = (summed * scale * norm[...]).astype(bf16)
    hidden = jnp.dot(normed, win[...], preferred_element_type=f32)
    hidden = (0.5 * hidden * (1.0 + lax.erf(hidden * math.sqrt(0.5)))).astype(bf16)
    result = summed + jnp.dot(hidden, wout[...], preferred_element_type=f32)
    res[...] = result.astype(bf16)
    back = pltpu.make_async_copy(res, out_hbm, local_sem.at[0])
    back.start()

    def first_done(g, carry):
        @pl.when(g != mine)
        def _():
            first_copy(g).wait_send()

        return carry

    lax.fori_loop(0, workers, first_done, 0)

    @pl.when(gives)
    def _():
        filt_copy.wait_send()

    for da, db in neighbours:
        @pl.when(inside(da))
        def _():
            halo_copy(da, db).wait_send()

    @pl.when(worker)
    def _():
        def second_done(o, carry):
            @pl.when(o != me)
            def _():
                second_copy(o).wait_send()

            return carry

        lax.fori_loop(0, devices, second_done, 0)

    back.wait()

    @pl.when(jnp.logical_not(worker))
    def _():
        for i in (2, 3, 4):
            fetch[i].wait()


def sphere_block(lat_devices, lon_devices, latent_field, spectral_filter, conv_weight, norm_gain, weight_in, weight_out):
    channels, lat_rows, lon_cols = latent_field.shape
    points = lat_rows * lon_cols
    workers = lat_devices * lon_devices // 2
    own = channels // workers
    up = upper_rows(own)
    table, select, quad, starts = folded_tables(lat_devices, lon_devices, lat_rows, lon_cols)
    table = jnp.asarray(table.astype(jnp.bfloat16))
    args = [
        jnp.transpose(latent_field, (1, 2, 0)).reshape(points, channels),
        spectral_filter.T,
        conv_weight,
        norm_gain[None, :],
        weight_in,
        weight_out,
        table,
        jnp.asarray(select),
        jnp.asarray(quad),
    ]
    order = [0, 1, 2, 3, 4, 5, 6, 7, 8]
    copies = [pltpu.VMEM(args[i].shape, args[i].dtype) for i in order]
    devices = lat_devices * lon_devices
    bf16, f32, dma = jnp.bfloat16, jnp.float32, pltpu.SemaphoreType.DMA
    scratch = [
        pltpu.VMEM((points, channels), f32),
        pltpu.VMEM((workers, up, 128), bf16),
        pltpu.VMEM((devices, up, 128), bf16),
        pltpu.VMEM((devices, up, 128), bf16),
        pltpu.VMEM((workers, up, 128), bf16),
        pltpu.VMEM(args[1].shape, f32),
        pltpu.VMEM((2, lat_rows, channels), bf16),
        pltpu.VMEM((4, 8, 128), bf16),
        pltpu.VMEM((4, lat_rows, channels), bf16),
        pltpu.VMEM((4, 8, 128), bf16),
        pltpu.VMEM((points, channels), f32),
        pltpu.VMEM((points, channels), bf16),
        dma((9,)), dma((workers,)), dma((devices,)), dma((devices,)), dma((workers,)),
        dma((8,)), dma((8,)), dma, dma,
    ]
    result = pl.pallas_call(
        functools.partial(block_kernel, lat_devices, lon_devices, lat_rows, lon_cols, starts),
        out_shape=jax.ShapeDtypeStruct((points, channels), bf16),
        in_specs=[pl.BlockSpec(memory_space=pl.ANY)] * 9,
        out_specs=pl.BlockSpec(memory_space=pl.ANY),
        scratch_shapes=copies + scratch,
        compiler_params=pltpu.CompilerParams(collective_id=0, has_side_effects=True),
        name="sphere_block",
    )(*args)
    return jnp.transpose(result.reshape(lat_rows, lon_cols, channels), (2, 0, 1))


def fits_block(lat_devices, lon_devices, latent_field):
    channels, lat_rows, lon_cols = latent_field.shape
    workers = lat_devices * lon_devices // 2
    return (
        lat_devices % 4 == 0
        and lon_devices % 4 == 0
        and lat_rows == 8
        and lon_cols == 8
        and channels % (8 * workers) == 0
        and channels % 128 == 0
        and channels <= 1024
    )


def block_or_banded(lat_devices, lon_devices, *arguments):
    if fits_block(lat_devices, lon_devices, arguments[0]):
        return sphere_block(lat_devices, lon_devices, *arguments)
    return on_device(*arguments)


def solution(mesh):
    return jax.shard_map(
        functools.partial(block_or_banded, mesh.shape["lat"], mesh.shape["lon"]),
        mesh=mesh,
        in_specs=(P(None, "lat", "lon"), P("lon", None), P(), P(), P(), P()),
        out_specs=P(None, "lat", "lon"),
        check_vma=False,
    )
```

profile of v0, /device:TPU:0, one launch (start us, length us, event | category | flops | bytes accessed | tf_op | source)
XLA Modules:
  0.0 22.2 jit_solution(10942863791121054736)
XLA Ops:
  0.0 1.3 %broadcast_in_dim.3.norm_hbm = f32[1,640]{1,0:T(1,128)} reshape(f32[640]{0:T(1024)} %param.12) | data formatting | bytes 5120 | tf_op jit(solution)/shard_map/broadcast_in_dim | solution.py:639
  1.3 19.4 %sphere_block.1 = bf16[64,640]{1,0:T(8,128)(2,1)} custom-call(bf16[64,640]{1,0:T(8,128)(2,1)} %bitcast.8, f32[32,80]{1,0:T(8,128)} %bitcast.9, f32[9,640]{1,0:T(8,128)} %taps_hbm.1, f32[1,640]{1,0:T(1,128)} %broadcast_in_dim.3.norm_hbm, bf16[640,1280]{1,0:T(8,128)(2,1)} %win_hbm.1, bf16[1280,640]{1,0:T(8,128)(2,1)} %wout_hbm.1, ...), custom_call_target="tpu_custom_call" | custom-call | tf_op jit(solution)/shard_map/sphere_block/pallas_call | solution.py:666
  20.7 1.5 %copy.11 = bf16[640,8,8]{0,2,1:T(8,128)(2,1)} copy(bf16[640,8,8]{0,2,1:T(8,128)(2,1)} %bitcast.7) | data formatting | bytes 163840
where the time goes:
time: 22.4 us; the launch traced here: 22.2 us
  Pallas kernels  19.4 us (87%)
  local copies, waits for them, and re-layouts  2.8 us (12%)
    pallas_call x1, Pallas kernels, sphere_block(): pl.pallas_call(functools.partial(block_kernel, lat_devices, lon_devices,...  19.4 us
    unnamed x1, local copies, waits for them, and re-layouts  1.53 us
    broadcast_in_dim x1, local copies, waits for them, and re-layouts, sphere_block(): norm_gain[None, :]  1.27 us

commit v1 on v0

--- a/solution.py
+++ b/solution.py
@@ -228,16 +228,12 @@
 NT = (((1,), (1,)), ((), ()))
 
 
-def upper_rows(own):
-    return -(-(own // 2) // 8) * 8
-
-
 def block_kernel(
     lat_devices, lon_devices, lat_rows, lon_cols, starts,
-    x_hbm, filter_hbm, taps_hbm, norm_hbm, win_hbm, wout_hbm, table_hbm, select_hbm, quad_hbm,
-    out_hbm,
-    xb, filt, taps, norm, win, wout, table, select, quad,
-    xf, src, mid, out, dst, filt_in, edge_out, corner_out, edge_in, corner_in, total, res,
+    x_hbm, filter_hbm, taps_hbm, norm_hbm, win_hbm, table_hbm, select_hbm, quad_hbm,
+    out_hbm, hid_hbm,
+    xb, filt, taps, norm, win, table, select, quad,
+    xf, src, mid, out, dst, filt_in, edge_out, corner_out, edge_in, corner_in, total, res, hid,
     local_sem, send1, recv1, send2, recv2, halo_send, halo_recv, filt_send, filt_recv,
 ):
     A, B = lat_devices, lon_devices
@@ -246,8 +242,8 @@
     devices = A * B
     points, channels = xb.shape
     own = channels // workers
-    up = upper_rows(own)
-    low = own - up
+    rows = own // 2
+    whole = rows // 8 * 8
     half = points
     a, b = lax.axis_index("lat"), lax.axis_index("lon")
     me = b * A + a
@@ -259,7 +255,7 @@
         pltpu.make_async_copy(s, d, local_sem.at[i])
         for i, (s, d) in enumerate(
             [(x_hbm, xb), (filter_hbm, filt), (quad_hbm, quad), (table_hbm, table), (select_hbm, select),
-             (taps_hbm, taps), (norm_hbm, norm), (win_hbm, win), (wout_hbm, wout)]
+             (taps_hbm, taps), (norm_hbm, norm), (win_hbm, win)]
         )
     ]
     fetch[0].start()
@@ -274,14 +270,16 @@
 
     @pl.when(worker)
     def _():
-        def greet(step, carry):
-            peer = lax.rem(me + step, devices)
-            pl.semaphore_signal(
-                barrier, inc=1, device_id=(lax.rem(peer, A), lax.div(peer, A)), device_id_type=MESH
-            )
+        def greet(peer, carry):
+            @pl.when(peer != me)
+            def _():
+                pl.semaphore_signal(
+                    barrier, inc=1, device_id=(lax.rem(peer, A), lax.div(peer, A)), device_id_type=MESH
+                )
+
             return carry
 
-        lax.fori_loop(1, devices, greet, 0)
+        lax.fori_loop(0, devices, greet, 0)
 
     @pl.when(jnp.logical_not(worker))
     def _():
@@ -306,22 +304,30 @@
     place = jnp.where(p_row == turned(lax.rem(p_col, half)), 1.0, 0.0)
     place_both = place.astype(bf16)
     place_left = jnp.where(p_col < half, place, 0.0).astype(bf16)
-    lane = lax.broadcasted_iota(jnp.int32, (up, 2 * half), 1)
-    left = lane < half
+    left = lax.broadcasted_iota(jnp.int32, (rows, 2 * half), 1) < half
+
+    def halves(value):
+        if rows == whole:
+            return value[:rows], value[rows:]
+        rest = value[2 * whole :]
+        return (
+            jnp.concatenate([value[:whole], rest[: rows - whole]], 0),
+            jnp.concatenate([value[whole : 2 * whole], rest[rows - whole :]], 0),
+        )
+
+    def joined(upper, lower):
+        pieces = [upper[:whole], lower[:whole]]
+        if rows > whole:
+            pieces += [upper[whole:], lower[whole:]]
+        return pieces
 
     fetch[0].wait()
     xf[...] = xb[...].astype(f32)
     xt = jnp.transpose(xf[...], (1, 0)).astype(bf16)
     xt = jnp.dot(xt, place_both, preferred_element_type=f32)
-    blank = jnp.zeros((up - low, 2 * half), f32)
     for g in range(workers):
-        upper = xt[own * g : own * g + up]
-        lower = jnp.concatenate([xt[own * g + up : own * (g + 1)], blank], 0)
+        upper, lower = halves(xt[own * g : own * (g + 1)])
         src[g] = jnp.where(left, upper, lower).astype(bf16)
-
-    @pl.when(worker)
-    def _():
-        mid[me] = src[mine]
 
     west, east = [
         jnp.concatenate([xf[k + lon_cols * r : k + lon_cols * r + 1] for r in range(lat_rows)], 0)
@@ -344,14 +350,20 @@
     greetings = greetings + rims * outside(0) + (1 + rims) * (outside(-1) + outside(1))
     pl.semaphore_wait(barrier, greetings)
 
+    zone = jnp.where(b < first, 0, jnp.where(worker, 1, 2))
+
     def first_copy(g):
         return pltpu.make_async_remote_copy(
-            src_ref=src.at[g], dst_ref=mid.at[me], send_sem=send1.at[g], recv_sem=recv1.at[me],
+            src_ref=src.at[g], dst_ref=mid.at[me], send_sem=send1, recv_sem=recv1.at[zone],
             device_id=(lax.rem(g, A), first + lax.div(g, A)), device_id_type=MESH,
         )
 
+    @pl.when(worker)
+    def _():
+        pltpu.make_async_copy(src.at[mine], mid.at[me], recv1.at[1]).start()
+
     def first_send(step, carry):
-        g = lax.rem(me + step, workers)
+        g = workers - 1 - step
 
         @pl.when(g != mine)
         def _():
@@ -383,16 +395,17 @@
         if db == 0:
             row = 0 if da < 0 else points - lon_cols
             source, target = xb.at[pl.ds(row, lon_cols)], edge_in.at[1 if da < 0 else 0]
-            slot = 1 if da < 0 else 0
+            kind = 0
         elif da == 0:
             slot = 3 if db < 0 else 2
             source, target = edge_out.at[0 if db < 0 else 1], edge_in.at[slot]
+            kind = 0
         else:
             index = (0 if da < 0 else 2) + (0 if db < 0 else 1)
             source, target = corner_out.at[index], corner_in.at[3 - index]
-            slot = 4 + 3 - index
+            kind = 1
         return pltpu.make_async_remote_copy(
-            src_ref=source, dst_ref=target, send_sem=halo_send.at[slot], recv_sem=halo_recv.at[slot],
+            src_ref=source, dst_ref=target, send_sem=halo_send.at[kind], recv_sem=halo_recv.at[kind],
             device_id=at(da, db), device_id_type=MESH,
         )
 
@@ -404,15 +417,9 @@
     def index_of(ai, bi):
         return bi * A + ai
 
-    def first_wait(o, carry):
-        @pl.when(o != me)
-        def _():
-            pltpu.make_async_remote_copy(
-                src_ref=src.at[0], dst_ref=mid.at[o], send_sem=send1.at[0], recv_sem=recv1.at[o],
-                device_id=(lax.rem(o, A), lax.div(o, A)), device_id_type=MESH,
-            ).wait_recv()
-
-        return carry
+    def arrived(zone, start, count):
+        blocks = mid.at[pl.ds(start, count)]
+        pltpu.make_async_copy(blocks, blocks, recv1.at[zone]).wait()
 
     def widths(c):
         return pl.ds(starts[c], starts[c + 1] - starts[c])
@@ -434,7 +441,7 @@
                     u, v = parts[ai][c], parts[ai + 1][c]
                     upper = jnp.where(left, u, pltpu.roll(v, half, 1))
                     lower = jnp.where(left, pltpu.roll(u, half, 1), v)
-                    tiles[c].append(jnp.concatenate([upper, lower[:low]], 0).astype(bf16))
+                    tiles[c].append(jnp.concatenate(joined(upper, lower), 0).astype(bf16))
         return [jnp.concatenate(t, 1) for t in tiles]
 
     inner = tuple(reversed(range(B2 // 2, B2)))
@@ -443,7 +450,7 @@
 
     def second_copy(o):
         return pltpu.make_async_remote_copy(
-            src_ref=out.at[o], dst_ref=dst.at[mine], send_sem=send2.at[o], recv_sem=recv2.at[mine],
+            src_ref=out.at[o], dst_ref=dst.at[mine], send_sem=send2, recv_sem=recv2,
             device_id=(lax.rem(o, A), lax.div(o, A)), device_id_type=MESH,
         )
 
@@ -466,13 +473,13 @@
         rows = lax.dot_general(pick, filt_in[...], NT, precision=highest, preferred_element_type=f32)
         gain = jnp.dot(rows, select[...], precision=highest, preferred_element_type=f32)
 
-        lax.fori_loop(A * inner[-1], A * (B - inner[-1]), first_wait, 0)
+        arrived(1, A * first, A * B2)
         acc = [
             jnp.dot(t, table[rows_of(inner), widths(i)], preferred_element_type=f32)
             for i, t in enumerate(folded(inner))
         ]
-        lax.fori_loop(0, A * inner[-1], first_wait, 0)
-        lax.fori_loop(A * (B - inner[-1]), devices, first_wait, 0)
+        arrived(0, 0, A * first)
+        arrived(2, A * (first + B2), A * (B - first - B2))
         for i, t in enumerate(folded(outer)):
             acc[i] = acc[i] + jnp.dot(t, table[rows_of(outer), widths(i)], preferred_element_type=f32)
         coef = [(acc[i] * gain[:, starts[i] : starts[i + 1]]).astype(bf16) for i in range(4)]
@@ -488,30 +495,24 @@
                     pp, mp, pm, mm = [g[:, at_lane : at_lane + 2 * half] for g in grid]
                     e0, e1, o0, o1 = pp + mp, pp - mp, pm + mm, pm - mm
                     for i, j, value in [(0, 0, e0 + o0), (1, 0, e1 + o1), (0, 1, e0 - o0), (1, 1, e1 - o1)]:
-                        upper = value[:up]
-                        lower = jnp.concatenate([value[up:], blank], 0)
+                        upper, lower = halves(value)
                         bj = B - 1 - bi if j else bi
                         a0, a1 = (A - 1 - ai, A - 2 - ai) if i else (ai, ai + 1)
                         out[index_of(a0, bj)] = jnp.where(left, upper, pltpu.roll(lower, half, 1)).astype(bf16)
                         out[index_of(a1, bj)] = jnp.where(left, pltpu.roll(upper, half, 1), lower).astype(bf16)
 
-            count = 2 * len(bs) * A
-
-            def second_send(step, carry):
-                t = lax.rem(me + step, count)
-                if bs == outer:
-                    o = t + jnp.where(t >= count // 2, devices - count, 0)
-                else:
-                    o = t + A * bs[-1]
-
+            def second_send(o, carry):
                 @pl.when(o != me)
                 def _():
                     second_copy(o).start()
 
                 return carry
 
-            lax.fori_loop(0, count, second_send, 0)
-        dst[mine] = out[me]
+            if bs == outer:
+                lax.fori_loop(0, A * first, second_send, 0)
+            else:
+                lax.fori_loop(A * first, devices, second_send, 0)
+        pltpu.make_async_copy(out.at[me], dst.at[mine], recv2).start()
 
     @pl.when(a == 0)
     def _():
@@ -525,10 +526,16 @@
         corner_in[2] = jnp.zeros(corner_in.shape[1:], bf16)
         corner_in[3] = jnp.zeros(corner_in.shape[1:], bf16)
 
-    for da, db in neighbours:
-        @pl.when(inside(-da))
-        def _():
-            halo_copy(da, db).wait_recv()
+    pole = rims == 1
+
+    def halo_wait(sems):
+        for edges, corners, case in [(3, 2, pole), (4, 4, jnp.logical_not(pole))]:
+            @pl.when(case)
+            def _():
+                for kind, blocks in enumerate([edge_in.at[pl.ds(0, edges)], corner_in.at[pl.ds(0, corners)]]):
+                    pltpu.make_async_copy(blocks, blocks, sems.at[kind]).wait()
+
+    halo_wait(halo_recv)
 
     fetch[5].wait()
     weight = taps[...]
@@ -557,66 +564,49 @@
         mix = mix.astype(bf16).astype(f32)
         total[pl.ds(lon_cols * r, lon_cols), :] = grid_rows[r + 1] + mix
 
-    for i in (6, 7, 8):
+    for i in (6, 7):
         fetch[i].wait()
 
-    def second_wait(g, carry):
-        @pl.when(g != mine)
-        def _():
-            pltpu.make_async_remote_copy(
-                src_ref=out.at[0], dst_ref=dst.at[g], send_sem=send2.at[0], recv_sem=recv2.at[g],
-                device_id=(lax.rem(g, A), first + lax.div(g, A)), device_id_type=MESH,
-            ).wait_recv()
-
-        return carry
-
-    lax.fori_loop(0, workers, second_wait, 0)
+    pltpu.make_async_copy(dst, dst, recv2).wait()
     parts = []
     for g in range(workers):
         piece = dst[g].astype(f32)
-        parts += [piece, pltpu.roll(piece, half, 1)[:low]]
+        parts += joined(piece, pltpu.roll(piece, half, 1))
     spectral = jnp.concatenate(parts, 0).astype(bf16)
     spectral = lax.dot_general(place_left, spectral, NT, preferred_element_type=f32)
     summed = (total[...] + spectral).astype(bf16).astype(f32)
     scale = lax.rsqrt(jnp.mean(summed * summed, axis=1, keepdims=True) + epsilon_norm)
-    normed = (summed * scale * norm[...]).astype(bf16)
+    normed = (summed * scale * norm[...][None, :]).astype(bf16)
     hidden = jnp.dot(normed, win[...], preferred_element_type=f32)
     hidden = (0.5 * hidden * (1.0 + lax.erf(hidden * math.sqrt(0.5)))).astype(bf16)
-    result = summed + jnp.dot(hidden, wout[...], preferred_element_type=f32)
-    res[...] = result.astype(bf16)
-    back = pltpu.make_async_copy(res, out_hbm, local_sem.at[0])
-    back.start()
-
-    def first_done(g, carry):
-        @pl.when(g != mine)
-        def _():
-            first_copy(g).wait_send()
-
-        return carry
-
-    lax.fori_loop(0, workers, first_done, 0)
+    res[...] = summed.astype(bf16)
+    hid[...] = hidden
+    back = [
+        pltpu.make_async_copy(res, out_hbm, local_sem.at[0]),
+        pltpu.make_async_copy(hid, hid_hbm, local_sem.at[1]),
+    ]
+    for copy in back:
+        copy.start()
+
+    def left_already(blocks, sem):
+        pltpu.make_async_copy(blocks, blocks, sem).wait()
+
+    @pl.when(worker)
+    def _():
+        left_already(src.at[pl.ds(0, workers - 1)], send1)
+        left_already(out.at[pl.ds(0, devices - 1)], send2)
+
+    @pl.when(jnp.logical_not(worker))
+    def _():
+        left_already(src, send1)
 
     @pl.when(gives)
     def _():
         filt_copy.wait_send()
 
-    for da, db in neighbours:
-        @pl.when(inside(da))
-        def _():
-            halo_copy(da, db).wait_send()
-
-    @pl.when(worker)
-    def _():
-        def second_done(o, carry):
-            @pl.when(o != me)
-            def _():
-                second_copy(o).wait_send()
-
-            return carry
-
-        lax.fori_loop(0, devices, second_done, 0)
-
-    back.wait()
+    halo_wait(halo_send)
+    for copy in back:
+        copy.wait()
 
     @pl.when(jnp.logical_not(worker))
     def _():
@@ -629,30 +619,28 @@
     points = lat_rows * lon_cols
     workers = lat_devices * lon_devices // 2
     own = channels // workers
-    up = upper_rows(own)
     table, select, quad, starts = folded_tables(lat_devices, lon_devices, lat_rows, lon_cols)
     table = jnp.asarray(table.astype(jnp.bfloat16))
     args = [
         jnp.transpose(latent_field, (1, 2, 0)).reshape(points, channels),
         spectral_filter.T,
         conv_weight,
-        norm_gain[None, :],
+        norm_gain,
         weight_in,
-        weight_out,
         table,
         jnp.asarray(select),
         jnp.asarray(quad),
     ]
-    order = [0, 1, 2, 3, 4, 5, 6, 7, 8]
+    order = range(len(args))
     copies = [pltpu.VMEM(args[i].shape, args[i].dtype) for i in order]
     devices = lat_devices * lon_devices
     bf16, f32, dma = jnp.bfloat16, jnp.float32, pltpu.SemaphoreType.DMA
     scratch = [
         pltpu.VMEM((points, channels), f32),
-        pltpu.VMEM((workers, up, 128), bf16),
-        pltpu.VMEM((devices, up, 128), bf16),
-        pltpu.VMEM((devices, up, 128), bf16),
-        pltpu.VMEM((workers, up, 128), bf16),
+        pltpu.VMEM((workers, own // 2, 128), bf16),
+        pltpu.VMEM((devices, own // 2, 128), bf16),
+        pltpu.VMEM((devices, own // 2, 128), bf16),
+        pltpu.VMEM((workers, own // 2, 128), bf16),
         pltpu.VMEM(args[1].shape, f32),
         pltpu.VMEM((2, lat_rows, channels), bf16),
         pltpu.VMEM((4, 8, 128), bf16),
@@ -660,18 +648,23 @@
         pltpu.VMEM((4, 8, 128), bf16),
         pltpu.VMEM((points, channels), f32),
         pltpu.VMEM((points, channels), bf16),
-        dma((9,)), dma((workers,)), dma((devices,)), dma((devices,)), dma((workers,)),
-        dma((8,)), dma((8,)), dma, dma,
+        pltpu.VMEM((points, weight_in.shape[1]), bf16),
+        dma((len(args),)), dma, dma((3,)), dma, dma, dma((2,)), dma((2,)), dma, dma,
     ]
-    result = pl.pallas_call(
+    summed, hidden = pl.pallas_call(
         functools.partial(block_kernel, lat_devices, lon_devices, lat_rows, lon_cols, starts),
-        out_shape=jax.ShapeDtypeStruct((points, channels), bf16),
-        in_specs=[pl.BlockSpec(memory_space=pl.ANY)] * 9,
-        out_specs=pl.BlockSpec(memory_space=pl.ANY),
+        out_shape=[
+            jax.ShapeDtypeStruct((points, channels), bf16),
+            jax.ShapeDtypeStruct((points, weight_in.shape[1]), bf16),
+        ],
+        in_specs=[pl.BlockSpec(memory_space=pl.ANY)] * len(args),
+        out_specs=[pl.BlockSpec(memory_space=pl.ANY)] * 2,
         scratch_shapes=copies + scratch,
         compiler_params=pltpu.CompilerParams(collective_id=0, has_side_effects=True),
         name="sphere_block",
     )(*args)
+    result = jnp.dot(hidden, weight_out, preferred_element_type=f32)
+    result = (summed.astype(f32) + result).astype(bf16)
     return jnp.transpose(result.reshape(lat_rows, lon_cols, channels), (2, 0, 1))
 
 
@@ -684,6 +677,7 @@
         and lat_rows == 8
         and lon_cols == 8
         and channels % (8 * workers) == 0
+        and channels // workers % 2 == 0
         and channels % 128 == 0
         and channels <= 1024
     )

time: 22.4 us -> 19.4 us (0.87)
  local copies, waits for them, and re-layouts: 2.8 us -> 0.01 us
  Pallas kernels: 19.4 us -> 17.2 us
  matrix products: 0 us -> 2.01 us
    pallas_call x1, Pallas kernels: 19.4 us -> 17.2 us  [sphere_block(): pl.pallas_call(functools.partial(block_kernel, lat_devices, lon_devices,...]
    dot_general x0 -> x1, matrix products: none -> 2.01 us  [sphere_block(): result = jnp.dot(hidden, weight_out, preferred_element_type=f32)]
    unnamed x1 -> x2, local copies, waits for them, and re-layouts: 1.53 us -> 0.01 us
    broadcast_in_dim x1 -> x0, local copies, waits for them, and re-layouts: 1.27 us -> none  [sphere_block(): norm_gain[None, :]]
where the time goes in v1:
time: 19.4 us; the launch traced here: 19.3 us
  Pallas kernels  17.2 us (89%)
  matrix products  2.01 us (10%)
    pallas_call x1, Pallas kernels, sphere_block(): pl.pallas_call(functools.partial(block_kernel, lat_devices, lon_devices,...  17.2 us
    dot_general x1, matrix products, sphere_block(): result = jnp.dot(hidden, weight_out, preferred_element_type=f32)  2.01 us

profile of v1, /device:TPU:0, one launch (start us, length us, event | category | flops | bytes accessed | tf_op | source)
XLA Modules:
  0.0 19.3 jit_solution(14111362920937295107)
XLA Ops:
  0.0 0.0 copy-start
  0.0 17.2 %sphere_block.1 = (bf16[64,640]{1,0:T(8,128)(2,1)}, bf16[64,1280]{1,0:T(8,128)(2,1)}) custom-call(bf16[64,640]{1,0:T(8,128)(2,1)} %bitcast.10, f32[32,80]{1,0:T(8,128)} %bitcast.11, f32[9,640]{1,0:T(8,128)} %taps_hbm.1, f32[640]{0:T(1024)} %norm_hbm.1, bf16[640,1280]{1,0:T(8,128)(2,1)} %win_hbm.1, bf16[512,1152]{1,0:T(8,128)(2,1)} %constant.6.clone.table_hbm, ...), custom_call_target="tpu_custom_call" | custom-call | tf_op jit(solution)/shard_map/sphere_block/pallas_call | solution.py:654
  17.3 0.0 copy-done
  17.3 2.0 %fusion.1 = bf16[640,8,8]{0,2,1:T(8,128)(2,1)} fusion(bf16[64,1280]{1,0:T(8,128)(2,1)} %get-tuple-element.8, bf16[1280,640]{1,0:T(8,128)(2,1)S(1)} %copy-done, bf16[64,640]{1,0:T(8,128)(2,1)} %get-tuple-element.7), kind=kOutput, calls=%fused_computation.2 | convolution fusion | flops 104980480 | bytes 1966080 | tf_op jit(solution)/shard_map/dot_general | solution.py:666
Async XLA Ops:
  0.0 17.3 %copy-start = (bf16[1280,640]{1,0:T(8,128)(2,1)S(1)}, bf16[1280,640]{1,0:T(8,128)(2,1)}, u32[]{:S(2)}) copy-start(bf16[1280,640]{1,0:T(8,128)(2,1)} %param.14) | copy-start | bytes 4915204

commit v2 on v1

--- a/solution.py
+++ b/solution.py
@@ -225,21 +225,28 @@
 
 
 MESH = pl.DeviceIdType.MESH
+
+
+def worker_columns(lon_devices):
+    return lon_devices // 4, lon_devices // 2
+
+
 NT = (((1,), (1,)), ((), ()))
 
 
 def block_kernel(
     lat_devices, lon_devices, lat_rows, lon_cols, starts,
-    x_hbm, filter_hbm, taps_hbm, norm_hbm, win_hbm, table_hbm, select_hbm, quad_hbm,
-    out_hbm, hid_hbm,
-    xb, filt, taps, norm, win, table, select, quad,
-    xf, src, mid, out, dst, filt_in, edge_out, corner_out, edge_in, corner_in, total, res, hid,
+    x_hbm, filter_hbm, taps_hbm, norm_hbm, win_hbm, wout_hbm, table_hbm, select_hbm, quad_hbm,
+    res,
+    xb, filt, taps, norm, win, wout, table, select, quad,
+    xf, src, mid, out, dst, filt_in, edge_out, corner_out, edge_in, corner_in, total,
     local_sem, send1, recv1, send2, recv2, halo_send, halo_recv, filt_send, filt_recv,
 ):
     A, B = lat_devices, lon_devices
-    A2, B2, first = A // 2, B // 2, B // 4
-    workers = A * B2
-    devices = A * B
+    A2, B2 = A // 2, B // 2
+    first, count = worker_columns(B)
+    workers, devices = A * count, A * B
+    groups = workers // B
     points, channels = xb.shape
     own = channels // workers
     rows = own // 2
@@ -247,7 +254,7 @@
     half = points
     a, b = lax.axis_index("lat"), lax.axis_index("lon")
     me = b * A + a
-    worker = jnp.logical_and(b >= first, b < first + B2)
+    worker = jnp.logical_and(b >= first, b < first + count)
     mine = jnp.where(worker, (b - first) * A + a, -1)
     f32, bf16 = jnp.float32, jnp.bfloat16
 
@@ -255,7 +262,7 @@
         pltpu.make_async_copy(s, d, local_sem.at[i])
         for i, (s, d) in enumerate(
             [(x_hbm, xb), (filter_hbm, filt), (quad_hbm, quad), (table_hbm, table), (select_hbm, select),
-             (taps_hbm, taps), (norm_hbm, norm), (win_hbm, win)]
+             (taps_hbm, taps), (norm_hbm, norm), (win_hbm, win), (wout_hbm, wout)]
         )
     ]
     fetch[0].start()
@@ -343,14 +350,15 @@
 
     def outside(db):
         other = lax.rem(b + db + B, B)
-        return jnp.where(jnp.logical_and(other >= first, other < first + B2), 0, 1)
+        return jnp.where(jnp.logical_and(other >= first, other < first + count), 0, 1)
 
     rims = jnp.where(a > 0, 1, 0) + jnp.where(a < A - 1, 1, 0)
     greetings = jnp.where(worker, workers - 1, workers)
     greetings = greetings + rims * outside(0) + (1 + rims) * (outside(-1) + outside(1))
     pl.semaphore_wait(barrier, greetings)
 
-    zone = jnp.where(b < first, 0, jnp.where(worker, 1, 2))
+    B4 = B2 // 2
+    zone = jnp.where(b < B4, 0, jnp.where(b < B - B4, 1, 2))
 
     def first_copy(g):
         return pltpu.make_async_remote_copy(
@@ -360,7 +368,7 @@
 
     @pl.when(worker)
     def _():
-        pltpu.make_async_copy(src.at[mine], mid.at[me], recv1.at[1]).start()
+        pltpu.make_async_copy(src.at[mine], mid.at[me], recv1.at[zone]).start()
 
     def first_send(step, carry):
         g = workers - 1 - step
@@ -374,8 +382,9 @@
     lax.fori_loop(0, workers, first_send, 0)
 
     fetch[1].wait()
-    owner_row = lax.div(a, A2) == lax.rem(b, 2)
-    filt_lon = first + lax.div(b, 2)
+    share = lax.rem(a + A * B - b * groups, A)
+    owner_row = share < groups
+    filt_lon = first + lax.div(b * groups + share, A)
     keeps = jnp.logical_and(owner_row, filt_lon == b)
     gives = jnp.logical_and(owner_row, filt_lon != b)
     filt_copy = pltpu.make_async_remote_copy(
@@ -463,23 +472,23 @@
         def _():
             pltpu.make_async_remote_copy(
                 src_ref=filt, dst_ref=filt_in, send_sem=filt_send, recv_sem=filt_recv,
-                device_id=(a, 2 * (b - first) + lax.div(a, A2)), device_id_type=MESH,
+                device_id=(a, lax.div(mine, groups)), device_id_type=MESH,
             ).wait_recv()
 
         held = filt_in.shape[1]
         r = lax.broadcasted_iota(jnp.int32, (own, held), 0)
         c = lax.broadcasted_iota(jnp.int32, (own, held), 1)
-        pick = jnp.where(c == r + lax.rem(a, A2) * own, 1.0, 0.0)
+        pick = jnp.where(c == r + lax.rem(mine, groups) * own, 1.0, 0.0)
         rows = lax.dot_general(pick, filt_in[...], NT, precision=highest, preferred_element_type=f32)
         gain = jnp.dot(rows, select[...], precision=highest, preferred_element_type=f32)
 
-        arrived(1, A * first, A * B2)
+        arrived(1, A * B4, devices - 2 * A * B4)
         acc = [
             jnp.dot(t, table[rows_of(inner), widths(i)], preferred_element_type=f32)
             for i, t in enumerate(folded(inner))
         ]
-        arrived(0, 0, A * first)
-        arrived(2, A * (first + B2), A * (B - first - B2))
+        arrived(0, 0, A * B4)
+        arrived(2, devices - A * B4, A * B4)
         for i, t in enumerate(folded(outer)):
             acc[i] = acc[i] + jnp.dot(t, table[rows_of(outer), widths(i)], preferred_element_type=f32)
         coef = [(acc[i] * gain[:, starts[i] : starts[i + 1]]).astype(bf16) for i in range(4)]
@@ -509,9 +518,9 @@
                 return carry
 
             if bs == outer:
-                lax.fori_loop(0, A * first, second_send, 0)
+                lax.fori_loop(0, A * B4, second_send, 0)
             else:
-                lax.fori_loop(A * first, devices, second_send, 0)
+                lax.fori_loop(A * B4, devices, second_send, 0)
         pltpu.make_async_copy(out.at[me], dst.at[mine], recv2).start()
 
     @pl.when(a == 0)
@@ -564,7 +573,7 @@
         mix = mix.astype(bf16).astype(f32)
         total[pl.ds(lon_cols * r, lon_cols), :] = grid_rows[r + 1] + mix
 
-    for i in (6, 7):
+    for i in (6, 7, 8):
         fetch[i].wait()
 
     pltpu.make_async_copy(dst, dst, recv2).wait()
@@ -579,14 +588,8 @@
     normed = (summed * scale * norm[...][None, :]).astype(bf16)
     hidden = jnp.dot(normed, win[...], preferred_element_type=f32)
     hidden = (0.5 * hidden * (1.0 + lax.erf(hidden * math.sqrt(0.5)))).astype(bf16)
-    res[...] = summed.astype(bf16)
-    hid[...] = hidden
-    back = [
-        pltpu.make_async_copy(res, out_hbm, local_sem.at[0]),
-        pltpu.make_async_copy(hid, hid_hbm, local_sem.at[1]),
-    ]
-    for copy in back:
-        copy.start()
+    result = summed + jnp.dot(hidden, wout[...], preferred_element_type=f32)
+    res[...] = result.astype(bf16)
 
     def left_already(blocks, sem):
         pltpu.make_async_copy(blocks, blocks, sem).wait()
@@ -605,8 +608,6 @@
         filt_copy.wait_send()
 
     halo_wait(halo_send)
-    for copy in back:
-        copy.wait()
 
     @pl.when(jnp.logical_not(worker))
     def _():
@@ -617,7 +618,7 @@
 def sphere_block(lat_devices, lon_devices, latent_field, spectral_filter, conv_weight, norm_gain, weight_in, weight_out):
     channels, lat_rows, lon_cols = latent_field.shape
     points = lat_rows * lon_cols
-    workers = lat_devices * lon_devices // 2
+    workers = lat_devices * worker_columns(lon_devices)[1]
     own = channels // workers
     table, select, quad, starts = folded_tables(lat_devices, lon_devices, lat_rows, lon_cols)
     table = jnp.asarray(table.astype(jnp.bfloat16))
@@ -627,6 +628,7 @@
         conv_weight,
         norm_gain,
         weight_in,
+        weight_out,
         table,
         jnp.asarray(select),
         jnp.asarray(quad),
@@ -647,30 +649,23 @@
         pltpu.VMEM((4, lat_rows, channels), bf16),
         pltpu.VMEM((4, 8, 128), bf16),
         pltpu.VMEM((points, channels), f32),
-        pltpu.VMEM((points, channels), bf16),
-        pltpu.VMEM((points, weight_in.shape[1]), bf16),
         dma((len(args),)), dma, dma((3,)), dma, dma, dma((2,)), dma((2,)), dma, dma,
     ]
-    summed, hidden = pl.pallas_call(
+    result = pl.pallas_call(
         functools.partial(block_kernel, lat_devices, lon_devices, lat_rows, lon_cols, starts),
-        out_shape=[
-            jax.ShapeDtypeStruct((points, channels), bf16),
-            jax.ShapeDtypeStruct((points, weight_in.shape[1]), bf16),
-        ],
+        out_shape=pltpu.VMEM((points, channels), bf16),
         in_specs=[pl.BlockSpec(memory_space=pl.ANY)] * len(args),
-        out_specs=[pl.BlockSpec(memory_space=pl.ANY)] * 2,
+        out_specs=pl.BlockSpec(memory_space=pltpu.VMEM),
         scratch_shapes=copies + scratch,
         compiler_params=pltpu.CompilerParams(collective_id=0, has_side_effects=True),
         name="sphere_block",
     )(*args)
-    result = jnp.dot(hidden, weight_out, preferred_element_type=f32)
-    result = (summed.astype(f32) + result).astype(bf16)
     return jnp.transpose(result.reshape(lat_rows, lon_cols, channels), (2, 0, 1))
 
 
 def fits_block(lat_devices, lon_devices, latent_field):
     channels, lat_rows, lon_cols = latent_field.shape
-    workers = lat_devices * lon_devices // 2
+    workers = lat_devices * worker_columns(lon_devices)[1]
     return (
         lat_devices % 4 == 0
         and lon_devices % 4 == 0

time: 19.4 us -> 17.6 us (0.907)
  matrix products: 2.01 us -> 0 us
  local copies, waits for them, and re-layouts: 0.01 us -> 0.64 us
  Pallas kernels: 17.2 us -> 16.8 us
    dot_general x1 -> x0, matrix products: 2.01 us -> none  [sphere_block(): result = jnp.dot(hidden, weight_out, preferred_element_type=f32)]
    unnamed x2 -> x1, local copies, waits for them, and re-layouts: 0.01 us -> 0.64 us
    pallas_call x1, Pallas kernels: 17.2 us -> 16.8 us  [sphere_block(): pl.pallas_call(functools.partial(block_kernel, lat_devices, lon_devices,...]
where the time goes in v2:
time: 17.6 us; the launch traced here: 17.5 us
  Pallas kernels  16.8 us (95%)
  local copies, waits for them, and re-layouts  0.64 us (4%)
    pallas_call x1, Pallas kernels, sphere_block(): pl.pallas_call(functools.partial(block_kernel, lat_devices, lon_devices,...  16.8 us
    unnamed x1, local copies, waits for them, and re-layouts  0.64 us

profile of v2, /device:TPU:0, one launch (start us, length us, event | category | flops | bytes accessed | tf_op | source)
XLA Modules:
  0.0 17.5 jit_solution(7578534066343913761)
XLA Ops:
  0.0 16.8 %sphere_block.1 = bf16[64,640]{1,0:T(8,128)(2,1)S(1)} custom-call(bf16[64,640]{1,0:T(8,128)(2,1)} %bitcast.8, f32[32,80]{1,0:T(8,128)} %bitcast.9, f32[9,640]{1,0:T(8,128)} %taps_hbm.1, f32[640]{0:T(1024)} %norm_hbm.1, bf16[640,1280]{1,0:T(8,128)(2,1)} %win_hbm.1, bf16[1280,640]{1,0:T(8,128)(2,1)} %wout_hbm.1, bf16[512,1152]{1,0:T(8,128)(2,1)} %constant.6.clone.table_hbm, ...), custom_call_target="tpu_custom_call" | custom-call | tf_op jit(solution)/shard_map/sphere_block/pallas_call | solution.py:654
  16.8 0.6 %copy.11 = bf16[640,8,8]{0,2,1:T(8,128)(2,1)} copy(bf16[640,8,8]{0,2,1:T(8,128)(2,1)S(1)} %bitcast.7) | data formatting | bytes 163840

commit v3 on v2

--- a/solution.py
+++ b/solution.py
@@ -418,6 +418,17 @@
             device_id=at(da, db), device_id_type=MESH,
         )
 
+    def left_already(blocks, sem):
+        pltpu.make_async_copy(blocks, blocks, sem).wait()
+
+    @pl.when(worker)
+    def _():
+        left_already(src.at[pl.ds(0, workers - 1)], send1)
+
+    @pl.when(jnp.logical_not(worker))
+    def _():
+        left_already(src, send1)
+
     for da, db in neighbours:
         @pl.when(inside(da))
         def _():
@@ -510,6 +521,10 @@
                         out[index_of(a0, bj)] = jnp.where(left, upper, pltpu.roll(lower, half, 1)).astype(bf16)
                         out[index_of(a1, bj)] = jnp.where(left, pltpu.roll(upper, half, 1), lower).astype(bf16)
 
+            def near_send(step, carry):
+                second_copy(lax.rem(step, B4) * A + lax.div(step, B4)).start()
+                return carry
+
             def second_send(o, carry):
                 @pl.when(o != me)
                 def _():
@@ -518,8 +533,9 @@
                 return carry
 
             if bs == outer:
-                lax.fori_loop(0, A * B4, second_send, 0)
+                lax.fori_loop(0, B4, near_send, 0)
             else:
+                lax.fori_loop(B4, A * B4, near_send, 0)
                 lax.fori_loop(A * B4, devices, second_send, 0)
         pltpu.make_async_copy(out.at[me], dst.at[mine], recv2).start()
 
@@ -591,17 +607,9 @@
     result = summed + jnp.dot(hidden, wout[...], preferred_element_type=f32)
     res[...] = result.astype(bf16)
 
-    def left_already(blocks, sem):
-        pltpu.make_async_copy(blocks, blocks, sem).wait()
-
     @pl.when(worker)
     def _():
-        left_already(src.at[pl.ds(0, workers - 1)], send1)
         left_already(out.at[pl.ds(0, devices - 1)], send2)
-
-    @pl.when(jnp.logical_not(worker))
-    def _():
-        left_already(src, send1)
 
     @pl.when(gives)
     def _():

time: 17.6 us -> 17.2 us (0.977)
  Pallas kernels: 16.8 us -> 16.4 us
    pallas_call x1, Pallas kernels: 16.8 us -> 16.4 us  [sphere_block(): pl.pallas_call(functools.partial(block_kernel, lat_devices, lon_devices,...]
where the time goes in v3:
time: 17.2 us; the launch traced here: 17.1 us
  Pallas kernels  16.4 us (95%)
  local copies, waits for them, and re-layouts  0.64 us (4%)
    pallas_call x1, Pallas kernels, sphere_block(): pl.pallas_call(functools.partial(block_kernel, lat_devices, lon_devices,...  16.4 us
    unnamed x1, local copies, waits for them, and re-layouts  0.64 us

profile of v3, /device:TPU:0, one launch (start us, length us, event | category | flops | bytes accessed | tf_op | source)
XLA Modules:
  0.0 17.1 jit_solution(17476309110112595886)
XLA Ops:
  0.0 16.4 %sphere_block.1 = bf16[64,640]{1,0:T(8,128)(2,1)S(1)} custom-call(bf16[64,640]{1,0:T(8,128)(2,1)} %bitcast.8, f32[32,80]{1,0:T(8,128)} %bitcast.9, f32[9,640]{1,0:T(8,128)} %taps_hbm.1, f32[640]{0:T(1024)} %norm_hbm.1, bf16[640,1280]{1,0:T(8,128)(2,1)} %win_hbm.1, bf16[1280,640]{1,0:T(8,128)(2,1)} %wout_hbm.1, bf16[512,1152]{1,0:T(8,128)(2,1)} %constant.6.clone.table_hbm, ...), custom_call_target="tpu_custom_call" | custom-call | tf_op jit(solution)/shard_map/sphere_block/pallas_call | solution.py:662
  16.4 0.6 %copy.11 = bf16[640,8,8]{0,2,1:T(8,128)(2,1)} copy(bf16[640,8,8]{0,2,1:T(8,128)(2,1)S(1)} %bitcast.7) | data formatting | bytes 163840

commit v4 on v3

--- a/solution.py
+++ b/solution.py
@@ -601,8 +601,8 @@
     spectral = lax.dot_general(place_left, spectral, NT, preferred_element_type=f32)
     summed = (total[...] + spectral).astype(bf16).astype(f32)
     scale = lax.rsqrt(jnp.mean(summed * summed, axis=1, keepdims=True) + epsilon_norm)
-    normed = (summed * scale * norm[...][None, :]).astype(bf16)
-    hidden = jnp.dot(normed, win[...], preferred_element_type=f32)
+    scaled = (summed * norm[...][None, :]).astype(bf16)
+    hidden = jnp.dot(scaled, win[...], preferred_element_type=f32) * scale
     hidden = (0.5 * hidden * (1.0 + lax.erf(hidden * math.sqrt(0.5)))).astype(bf16)
     result = summed + jnp.dot(hidden, wout[...], preferred_element_type=f32)
     res[...] = result.astype(bf16)

time: 17.2 us -> 17.1 us (level)
  no operation moved by 1% of the time
where the time goes in v4:
time: 17.1 us; the launch traced here: 16.9 us
  Pallas kernels  16.3 us (95%)
  local copies, waits for them, and re-layouts  0.64 us (4%)
    pallas_call x1, Pallas kernels, sphere_block(): pl.pallas_call(functools.partial(block_kernel, lat_devices, lon_devices,...  16.3 us
    unnamed x1, local copies, waits for them, and re-layouts  0.64 us

profile of v4, /device:TPU:0, one launch (start us, length us, event | category | flops | bytes accessed | tf_op | source)
XLA Modules:
  0.0 16.9 jit_solution(11246666981934397606)
XLA Ops:
  0.0 16.3 %sphere_block.1 = bf16[64,640]{1,0:T(8,128)(2,1)S(1)} custom-call(bf16[64,640]{1,0:T(8,128)(2,1)} %bitcast.8, f32[32,80]{1,0:T(8,128)} %bitcast.9, f32[9,640]{1,0:T(8,128)} %taps_hbm.1, f32[640]{0:T(1024)} %norm_hbm.1, bf16[640,1280]{1,0:T(8,128)(2,1)} %win_hbm.1, bf16[1280,640]{1,0:T(8,128)(2,1)} %wout_hbm.1, bf16[512,1152]{1,0:T(8,128)(2,1)} %constant.6.clone.table_hbm, ...), custom_call_target="tpu_custom_call" | custom-call | tf_op jit(solution)/shard_map/sphere_block/pallas_call | solution.py:662
  16.3 0.6 %copy.11 = bf16[640,8,8]{0,2,1:T(8,128)(2,1)} copy(bf16[640,8,8]{0,2,1:T(8,128)(2,1)S(1)} %bitcast.7) | data formatting | bytes 163840

commit v5 on v4

--- a/solution.py
+++ b/solution.py
@@ -227,8 +227,11 @@
 MESH = pl.DeviceIdType.MESH
 
 
-def worker_columns(lon_devices):
-    return lon_devices // 4, lon_devices // 2
+def worker_places(lat_devices, lon_devices):
+    quarter = lon_devices // 4
+    second = [(a, b) for b in range(quarter, 2 * quarter) for a in range(lat_devices)]
+    third = [(a, b) for b in range(2 * quarter, 3 * quarter) for a in range(lat_devices - 1)]
+    return [(0, b) for b in range(quarter)] + second + third
 
 
 NT = (((1,), (1,)), ((), ()))
@@ -240,12 +243,12 @@
     res,
     xb, filt, taps, norm, win, wout, table, select, quad,
     xf, src, mid, out, dst, filt_in, edge_out, corner_out, edge_in, corner_in, total,
-    local_sem, send1, recv1, send2, recv2, halo_send, halo_recv, filt_send, filt_recv,
+    local_sem, send1, recv1, send2, recv2, halo_send, halo_recv, filt_send, filt_recv, wrap,
 ):
     A, B = lat_devices, lon_devices
     A2, B2 = A // 2, B // 2
-    first, count = worker_columns(B)
-    workers, devices = A * count, A * B
+    places = worker_places(A, B)
+    workers, devices = len(places), A * B
     groups = workers // B
     points, channels = xb.shape
     own = channels // workers
@@ -254,8 +257,22 @@
     half = points
     a, b = lax.axis_index("lat"), lax.axis_index("lon")
     me = b * A + a
-    worker = jnp.logical_and(b >= first, b < first + count)
-    mine = jnp.where(worker, (b - first) * A + a, -1)
+    quarter = B // 4
+
+    def works(a, b):
+        z = lax.div(b, quarter)
+        return jnp.logical_or(
+            z == 1, jnp.logical_or(jnp.logical_and(z == 2, a < A - 1), jnp.logical_and(z == 0, a == 0))
+        )
+
+    worker = works(a, b)
+    mine = jnp.where(
+        b < quarter,
+        b,
+        quarter
+        + jnp.where(b < 2 * quarter, (b - quarter) * A + a, quarter * A + (b - 2 * quarter) * (A - 1) + a),
+    )
+    mine = jnp.where(worker, mine, -1)
     f32, bf16 = jnp.float32, jnp.bfloat16
 
     fetch = [
@@ -291,7 +308,7 @@
     @pl.when(jnp.logical_not(worker))
     def _():
         for da, db in neighbours:
-            @pl.when(inside(da))
+            @pl.when(jnp.logical_and(inside(da), b < B - 1) if db > 0 else inside(da))
             def _():
                 pl.semaphore_signal(barrier, inc=1, device_id=at(da, db), device_id_type=MESH)
 
@@ -348,14 +365,22 @@
         parts.append(jnp.zeros((8 - chunks, 128), f32))
         corner_out[i] = jnp.concatenate(parts, 0).astype(bf16)
 
-    def outside(db):
-        other = lax.rem(b + db + B, B)
-        return jnp.where(jnp.logical_and(other >= first, other < first + count), 0, 1)
-
     rims = jnp.where(a > 0, 1, 0) + jnp.where(a < A - 1, 1, 0)
     greetings = jnp.where(worker, workers - 1, workers)
-    greetings = greetings + rims * outside(0) + (1 + rims) * (outside(-1) + outside(1))
+    for da, db in neighbours:
+        other = at(da, db)
+        known = jnp.logical_and(inside(da), jnp.logical_not(works(*other)))
+        if db < 0:
+            known = jnp.logical_and(known, b > 0)
+        greetings = greetings + jnp.where(known, 1, 0)
     pl.semaphore_wait(barrier, greetings)
+
+    @pl.when(b == B - 1)
+    def _():
+        for da in (-1, 0, 1):
+            @pl.when(inside(da))
+            def _():
+                pl.semaphore_signal(wrap, inc=1, device_id=(a + da, 0), device_id_type=MESH)
 
     B4 = B2 // 2
     zone = jnp.where(b < B4, 0, jnp.where(b < B - B4, 1, 2))
@@ -363,38 +388,36 @@
     def first_copy(g):
         return pltpu.make_async_remote_copy(
             src_ref=src.at[g], dst_ref=mid.at[me], send_sem=send1, recv_sem=recv1.at[zone],
-            device_id=(lax.rem(g, A), first + lax.div(g, A)), device_id_type=MESH,
+            device_id=places[g], device_id_type=MESH,
         )
 
     @pl.when(worker)
     def _():
         pltpu.make_async_copy(src.at[mine], mid.at[me], recv1.at[zone]).start()
 
-    def first_send(step, carry):
-        g = workers - 1 - step
-
-        @pl.when(g != mine)
+    for order, case in [(reversed(range(workers)), b < B2), (range(workers), b >= B2)]:
+        for g in order:
+            @pl.when(jnp.logical_and(mine != g, case))
+            def _():
+                first_copy(g).start()
+
+    fetch[1].wait()
+    def filt_copy(g):
+        return pltpu.make_async_remote_copy(
+            src_ref=filt, dst_ref=filt_in, send_sem=filt_send.at[g % groups], recv_sem=filt_recv,
+            device_id=places[g], device_id_type=MESH,
+        )
+
+    givers, keeps = [], False
+    for g, (ag, bg) in enumerate(places):
+        if bg == g // groups:
+            keeps = jnp.logical_or(keeps, mine == g)
+        else:
+            givers.append((g, me == (g // groups) * A + ag))
+    for g, gives in givers:
+        @pl.when(gives)
         def _():
-            first_copy(g).start()
-
-        return carry
-
-    lax.fori_loop(0, workers, first_send, 0)
-
-    fetch[1].wait()
-    share = lax.rem(a + A * B - b * groups, A)
-    owner_row = share < groups
-    filt_lon = first + lax.div(b * groups + share, A)
-    keeps = jnp.logical_and(owner_row, filt_lon == b)
-    gives = jnp.logical_and(owner_row, filt_lon != b)
-    filt_copy = pltpu.make_async_remote_copy(
-        src_ref=filt, dst_ref=filt_in, send_sem=filt_send, recv_sem=filt_recv,
-        device_id=(a, filt_lon), device_id_type=MESH,
-    )
-
-    @pl.when(gives)
-    def _():
-        filt_copy.start()
+            filt_copy(g).start()
 
     @pl.when(keeps)
     def _():
@@ -428,6 +451,10 @@
     @pl.when(jnp.logical_not(worker))
     def _():
         left_already(src, send1)
+
+    @pl.when(b == 0)
+    def _():
+        pl.semaphore_wait(wrap, 1 + rims)
 
     for da, db in neighbours:
         @pl.when(inside(da))
@@ -481,10 +508,7 @@
 
         @pl.when(jnp.logical_not(keeps))
         def _():
-            pltpu.make_async_remote_copy(
-                src_ref=filt, dst_ref=filt_in, send_sem=filt_send, recv_sem=filt_recv,
-                device_id=(a, lax.div(mine, groups)), device_id_type=MESH,
-            ).wait_recv()
+            pltpu.make_async_copy(filt, filt_in, filt_recv).wait()
 
         held = filt_in.shape[1]
         r = lax.broadcasted_iota(jnp.int32, (own, held), 0)
@@ -522,7 +546,12 @@
                         out[index_of(a1, bj)] = jnp.where(left, pltpu.roll(upper, half, 1), lower).astype(bf16)
 
             def near_send(step, carry):
-                second_copy(lax.rem(step, B4) * A + lax.div(step, B4)).start()
+                o = lax.rem(step, B4) * A + lax.div(step, B4)
+
+                @pl.when(o != me)
+                def _():
+                    second_copy(o).start()
+
                 return carry
 
             def second_send(o, carry):
@@ -532,11 +561,24 @@
 
                 return carry
 
-            if bs == outer:
-                lax.fori_loop(0, B4, near_send, 0)
-            else:
-                lax.fori_loop(B4, A * B4, near_send, 0)
-                lax.fori_loop(A * B4, devices, second_send, 0)
+            def far_send(step, carry):
+                return second_send(A * (B - B4) - 1 - step, carry)
+
+            @pl.when(b < quarter)
+            def _():
+                if bs == outer:
+                    lax.fori_loop(A * (B - B4), devices, second_send, 0)
+                else:
+                    lax.fori_loop(0, A * (B - B4), far_send, 0)
+
+            @pl.when(b >= quarter)
+            def _():
+                if bs == outer:
+                    lax.fori_loop(0, B4, near_send, 0)
+                else:
+                    lax.fori_loop(B4, A * B4, near_send, 0)
+                    lax.fori_loop(A * B4, devices, second_send, 0)
+
         pltpu.make_async_copy(out.at[me], dst.at[mine], recv2).start()
 
     @pl.when(a == 0)
@@ -611,9 +653,10 @@
     def _():
         left_already(out.at[pl.ds(0, devices - 1)], send2)
 
-    @pl.when(gives)
-    def _():
-        filt_copy.wait_send()
+    for g, gives in givers:
+        @pl.when(gives)
+        def _():
+            filt_copy(g).wait_send()
 
     halo_wait(halo_send)
 
@@ -626,7 +669,7 @@
 def sphere_block(lat_devices, lon_devices, latent_field, spectral_filter, conv_weight, norm_gain, weight_in, weight_out):
     channels, lat_rows, lon_cols = latent_field.shape
     points = lat_rows * lon_cols
-    workers = lat_devices * worker_columns(lon_devices)[1]
+    workers = len(worker_places(lat_devices, lon_devices))
     own = channels // workers
     table, select, quad, starts = folded_tables(lat_devices, lon_devices, lat_rows, lon_cols)
     table = jnp.asarray(table.astype(jnp.bfloat16))
@@ -657,7 +700,8 @@
         pltpu.VMEM((4, lat_rows, channels), bf16),
         pltpu.VMEM((4, 8, 128), bf16),
         pltpu.VMEM((points, channels), f32),
-        dma((len(args),)), dma, dma((3,)), dma, dma, dma((2,)), dma((2,)), dma, dma,
+        dma((len(args),)), dma, dma((3,)), dma, dma, dma((2,)), dma((2,)), dma((workers // lon_devices,)), dma,
+        pltpu.SemaphoreType.REGULAR,
     ]
     result = pl.pallas_call(
         functools.partial(block_kernel, lat_devices, lon_devices, lat_rows, lon_cols, starts),
@@ -673,7 +717,7 @@
 
 def fits_block(lat_devices, lon_devices, latent_field):
     channels, lat_rows, lon_cols = latent_field.shape
-    workers = lat_devices * worker_columns(lon_devices)[1]
+    workers = len(worker_places(lat_devices, lon_devices))
     return (
         lat_devices % 4 == 0
         and lon_devices % 4 == 0

time: 17.1 us -> 16.7 us (0.977)
  Pallas kernels: 16.3 us -> 16 us
    pallas_call x1, Pallas kernels: 16.3 us -> 16 us  [sphere_block(): pl.pallas_call(functools.partial(block_kernel, lat_devices, lon_devices,...]
where the time goes in v5:
time: 16.7 us; the launch traced here: 16.6 us
  Pallas kernels  16 us (96%)
  local copies, waits for them, and re-layouts  0.64 us (4%)
    pallas_call x1, Pallas kernels, sphere_block(): pl.pallas_call(functools.partial(block_kernel, lat_devices, lon_devices,...  16 us
    unnamed x1, local copies, waits for them, and re-layouts  0.64 us

profile of v5, /device:TPU:0, one launch (start us, length us, event | category | flops | bytes accessed | tf_op | source)
XLA Modules:
  0.0 16.6 jit_solution(3088627951471499123)
XLA Ops:
  0.0 16.0 %sphere_block.1 = bf16[64,640]{1,0:T(8,128)(2,1)S(1)} custom-call(bf16[64,640]{1,0:T(8,128)(2,1)} %bitcast.8, f32[32,80]{1,0:T(8,128)} %bitcast.9, f32[9,640]{1,0:T(8,128)} %taps_hbm.1, f32[640]{0:T(1024)} %norm_hbm.1, bf16[640,1280]{1,0:T(8,128)(2,1)} %win_hbm.1, bf16[1280,640]{1,0:T(8,128)(2,1)} %wout_hbm.1, bf16[512,1152]{1,0:T(8,128)(2,1)} %constant.6.clone.table_hbm, ...), custom_call_target="tpu_custom_call" | custom-call | tf_op jit(solution)/shard_map/sphere_block/pallas_call | solution.py:706
  16.0 0.6 %copy.11 = bf16[640,8,8]{0,2,1:T(8,128)(2,1)} copy(bf16[640,8,8]{0,2,1:T(8,128)(2,1)S(1)} %bitcast.7) | data formatting | bytes 163840

commit v6 on v5

--- a/solution.py
+++ b/solution.py
@@ -444,10 +444,6 @@
     def left_already(blocks, sem):
         pltpu.make_async_copy(blocks, blocks, sem).wait()
 
-    @pl.when(worker)
-    def _():
-        left_already(src.at[pl.ds(0, workers - 1)], send1)
-
     @pl.when(jnp.logical_not(worker))
     def _():
         left_already(src, send1)
@@ -652,6 +648,7 @@
     @pl.when(worker)
     def _():
         left_already(out.at[pl.ds(0, devices - 1)], send2)
+        left_already(src.at[pl.ds(0, workers - 1)], send1)
 
     for g, gives in givers:
         @pl.when(gives)

time: 16.7 us -> 16.7 us (level)
  no operation moved by 1% of the time
where the time goes in v6:
time: 16.7 us; the launch traced here: 16.5 us
  Pallas kernels  15.9 us (95%)
  local copies, waits for them, and re-layouts  0.64 us (4%)
    pallas_call x1, Pallas kernels, sphere_block(): pl.pallas_call(functools.partial(block_kernel, lat_devices, lon_devices,...  15.9 us
    unnamed x1, local copies, waits for them, and re-layouts  0.64 us

profile of v6, /device:TPU:0, one launch (start us, length us, event | category | flops | bytes accessed | tf_op | source)
XLA Modules:
  0.0 16.5 jit_solution(15138438329655425359)
XLA Ops:
  0.0 15.9 %sphere_block.1 = bf16[64,640]{1,0:T(8,128)(2,1)S(1)} custom-call(bf16[64,640]{1,0:T(8,128)(2,1)} %bitcast.8, f32[32,80]{1,0:T(8,128)} %bitcast.9, f32[9,640]{1,0:T(8,128)} %taps_hbm.1, f32[640]{0:T(1024)} %norm_hbm.1, bf16[640,1280]{1,0:T(8,128)(2,1)} %win_hbm.1, bf16[1280,640]{1,0:T(8,128)(2,1)} %wout_hbm.1, bf16[512,1152]{1,0:T(8,128)(2,1)} %constant.6.clone.table_hbm, ...), custom_call_target="tpu_custom_call" | custom-call | tf_op jit(solution)/shard_map/sphere_block/pallas_call | solution.py:703
  15.9 0.6 %copy.11 = bf16[640,8,8]{0,2,1:T(8,128)(2,1)} copy(bf16[640,8,8]{0,2,1:T(8,128)(2,1)S(1)} %bitcast.7) | data formatting | bytes 163840
